TPU v7x, 32 devices: a whole 2x2x4 slice. The times are simulated.
32 devices in a mesh: row: 8 (over y, x, core), col: 4 (over z).
Axes of the slice: x: 2, y: 2, z: 4, core: 2. Of those that a mesh axis runs over, the one named last changes fastest.
Arguments:
- expression: bfloat16 [4096, 1024], P(('row', 'col')), may hold values from -200 to 200, as said below
- powers: int32 [10], replicated, may hold values from 1 to 20
Outputs:
- log_degree: float32 [10, 4096], P(None, ('row', 'col'))
- degree_freq: float32 [10, 10], replicated
- fit_slope: float32 [10], replicated
- mean_log: float32 [10], replicated
Inputs may be any that keep to these rules, and one draw needn't show every extreme that they name: Finite expression values.
All inputs are finite; a program needn't handle non-finite values.
Results may differ from a plain program's by a relative error of at most 0.0003.
Values may be sent and summed in bfloat16 or wider, within the bound.
A program may use at most 64 MiB of HBM per device.

v0:
```python
import jax
import jax.numpy as jnp
from jax import lax
from jax.sharding import PartitionSpec as P

BINS = 10


def gene_stats(genes):
    values = genes.astype(jnp.float32)
    gene_mean = jnp.mean(values, axis=1)
    centred = values - gene_mean[:, None]
    gene_inv = lax.rsqrt(jnp.mean(centred * centred, axis=1) + 1e-06)
    return (gene_mean, gene_inv)


def add_slice(totals, addend, start):
    current = lax.dynamic_slice_in_dim(totals, start, addend.shape[1], 1)
    return lax.dynamic_update_slice_in_dim(totals, current + addend, start, 1)


def block_sums(left_genes, right_genes, exponents, row_list, carry, left_start):
    row_count = left_genes.shape[0]
    block_rows = 256
    samples = left_genes.shape[1]
    left_mean, left_inv = gene_stats(left_genes)
    right_mean, right_inv = gene_stats(right_genes)

    def one_block(block_index, totals):
        row_totals, column_totals = totals
        offset = block_index * block_rows
        row_block = lax.dynamic_slice_in_dim(left_genes, offset, block_rows, 0)
        block_mean = lax.dynamic_slice_in_dim(left_mean, offset, block_rows, 0)
        block_inv = lax.dynamic_slice_in_dim(left_inv, offset, block_rows, 0)
        raw = lax.dot_general(
            row_block, right_genes, (((1,), (1,)), ((), ())), preferred_element_type=jnp.float32
        )
        pearson = (
            (raw / samples - block_mean[:, None] * right_mean[None, :])
            * block_inv[:, None]
            * right_inv[None, :]
        )
        log_abs = jnp.log(jnp.abs(pearson))
        row_parts = []
        for power_index in row_list:
            row_parts.append(jnp.sum(jnp.exp(exponents[power_index] * log_abs), axis=1))
        if row_parts:
            row_totals = add_slice(row_totals, jnp.stack(row_parts), left_start + offset)
        return (row_totals, column_totals)

    return lax.fori_loop(0, row_count // block_rows, one_block, carry)


def on_device(expression, powers):
    exponents = powers.astype(jnp.float32)
    npower = powers.shape[0]
    local_genes = expression.shape[0]
    row_width = local_genes * lax.axis_size("col")
    column_width = local_genes * lax.axis_size("row")
    row_list = list(range(npower))
    col_list = []
    initial = (
        jnp.zeros((len(row_list), row_width), jnp.float32),
        jnp.zeros((max(len(col_list), 1), column_width), jnp.float32),
    )
    left_genes = lax.all_gather(expression, "col", axis=0, tiled=True)
    row_totals, column_totals = block_sums(
        left_genes,
        lax.all_gather(expression, "row", axis=0, tiled=True),
        exponents,
        row_list,
        initial,
        0,
    )
    degree = lax.psum_scatter(row_totals, "col", scatter_dimension=1, tiled=True)
    peak = lax.pmax(jnp.max(degree, axis=1), ("row", "col"))
    position = jnp.clip(BINS * degree / peak[:, None] - 0.5, 0.0, BINS - 1.0)
    centres = jnp.arange(BINS, dtype=jnp.float32)
    weights = jnp.maximum(0.0, 1.0 - jnp.abs(position[:, :, None] - centres[None, None, :]))
    freq_total, degree_total = lax.psum(
        (jnp.sum(weights, axis=1), jnp.sum(degree, axis=1)), ("row", "col")
    )
    genes_all = local_genes * lax.axis_size("row") * lax.axis_size("col")
    degree_freq = freq_total / genes_all
    mean_log = jnp.log10(degree_total / genes_all)
    xfit = jnp.log10((centres[None, :] + 0.5) * peak[:, None] / BINS)
    yfit = jnp.log10(degree_freq + 1.0 / genes_all)
    xdev = xfit - jnp.mean(xfit, axis=1, keepdims=True)
    ydev = yfit - jnp.mean(yfit, axis=1, keepdims=True)
    fit_slope = jnp.sum(xdev * ydev, axis=1) / jnp.sum(xdev * xdev, axis=1)
    return (jnp.log10(degree), degree_freq, fit_slope, mean_log)


def solution(mesh):
    return jax.shard_map(
        on_device,
        mesh=mesh,
        in_specs=(P(("row", "col"), None), P()),
        out_specs=(P(None, ("row", "col")), P(), P(), P()),
        check_vma=False,
    )
```

profile of v0, /device:TPU:0, one launch (start us, length us, event | category | flops | bytes accessed | tf_op | source)
XLA Modules:
  0.0 201.4 jit_solution(1471055572352535315)
XLA Ops:
  7.2 0.0 all-gather.3.cloned.1.call-start
  7.2 0.7 all-gather.3.cloned.1.call-update
  7.9 0.0 all-gather.5.cloned.1.call-start
  7.9 0.7 all-gather.5.cloned.1.call-update
  8.6 0.0 reduce-scatter.2.cloned.1.call-start
  8.7 0.7 convert_element_type.9
  9.4 30.9 %all-gather.3.cloned.1.call-done = bf16[512,1024]{1,0:T(8,128)(2,1)} async-done(((bf16[128,1024]{1,0:T(8,128)(2,1)}), bf16[512,1024]{1,0:T(8,128)(2,1)}) %all-gather.3.cloned.1.call-update) | async-done | bytes 1048592 | tf_op jit(solution)/shard_map/all_gather | solution.py:66
  40.3 1.4 convert_reduce_fusion.1
  41.7 1.6 fusion.10
  43.4 26.0 %all-gather.5.cloned.1.call-done = bf16[1024,1024]{1,0:T(8,128)(2,1)} async-done(((bf16[128,1024]{1,0:T(8,128)(2,1)}), bf16[1024,1024]{1,0:T(8,128)(2,1)}) %all-gather.5.cloned.1.call-update) | async-done | bytes 2097168 | tf_op jit(solution)/shard_map/all_gather | solution.py:69
  69.4 0.0 copy-start
  69.4 0.0 copy-start.1
  69.4 2.1 %convert_reduce_fusion = f32[1024]{0:T(1024)S(1)} fusion(bf16[1024,1024]{1,0:T(8,128)(2,1)} %all-gather.5.cloned.1.call-done), kind=kLoop, calls=%fused_computation.20 | loop fusion | flops 2096128 | bytes 2101248 | tf_op jit(solution)/shard_map/reduce_sum | solution.py:11
  71.5 0.1 copy-done
  71.6 0.7 fusion.8
  72.3 0.0 copy-done.1
  72.3 19.4 %while.13 = (s32[]{:T(128)}, f32[10,512]{1,0:T(8,128)S(1)}, f32[10]{0:T(128)S(1)}, bf16[512,1024]{1,0:T(8,128)(2,1)S(1)}, bf16[1024,1024]{1,0:T(8,128)(2,1)S(1)}...) while((s32[]{:T(128)}, f32[10,512]{1,0:T(8,128)S(1)}, ...), condition=%wide.region_15.0_spmd, body=%wide.region_4.0_spmd.sunk | while | flops 543686656 | bytes 2715955 | solution.py:51
  72.3 0.1 dynamic_slice.39
  72.4 0.1 dynamic_slice.40
  72.5 0.7 fusion.20
  73.2 8.8 %exponential_reduce_fusion.11 = (f32[256]{0:T(256)S(1)}, f32[256]{0:T(256)S(1)}, f32[256]{0:T(256)S(1)}, f32[256]{0:T(256)S(1)}, f32[256]{0:T(256)S(1)}, /*index...) fusion(f32[]{:T(128)} %bitcast.43, f32[]{:T(128)} %bitcast.44, ...), kind=kOutput, calls=%fused_computation.6.clone.1 | convolution fusion | flops 543684096 | bytes 2641964 | tf_op jit(solution)/shard_map/while/body/eval_jaxpr/dot_general | solution.py:35
  81.9 0.1 stack.78
  82.0 0.1 dynamic_slice.39
  82.1 0.1 dynamic_slice.40
  82.2 0.7 fusion.20
  82.9 8.8 %exponential_reduce_fusion.11 = (f32[256]{0:T(256)S(1)}, f32[256]{0:T(256)S(1)}, f32[256]{0:T(256)S(1)}, f32[256]{0:T(256)S(1)}, f32[256]{0:T(256)S(1)}, /*index...) fusion(f32[]{:T(128)} %bitcast.43, f32[]{:T(128)} %bitcast.44, ...), kind=kOutput, calls=%fused_computation.6.clone.1 | convolution fusion | flops 543684096 | bytes 2641964 | tf_op jit(solution)/shard_map/while/body/eval_jaxpr/dot_general | solution.py:35
  91.6 0.1 stack.78
  91.7 0.0 copy-start.2
  91.7 0.6 copy-done.2
  92.3 0.0 reduce-scatter.2.cloned.1.call-update
  92.4 19.3 %reduce-scatter.2.cloned.1.call-done = f32[10,128]{1,0:T(8,128)} async-done(((f32[10,512]{1,0:T(8,128)}), f32[10,128]{1,0:T(8,128)}) %reduce-scatter.2.cloned.1.call-update) | async-done | bytes 5136 | tf_op jit(solution)/shard_map/reduce_scatter | solution.py:75
  111.7 0.8 fusion.14
  112.5 38.4 %pmax.7 = f32[10]{0:T(128)S(1)} all-reduce(f32[10]{0:T(128)S(1)} %get-tuple-element.170), channel_id=1, replica_groups=mesh['row'=8,'col'=4] {'row','col'}, use_global_device_ids=true, to_apply=%region_18.0 | all-reduce | flops 10 | bytes 80 | tf_op jit(solution)/shard_map/pmax | solution.py:76
  150.9 1.3 add_clamp_fusion
  152.2 0.1 maximum_reduce_fusion
  152.3 40.9 %all-reduce = (f32[10,10]{1,0:T(8,128)S(1)}, f32[10]{0:T(128)S(1)}) all-reduce(f32[10,10]{1,0:T(8,128)S(1)} %maximum_reduce_fusion, f32[10]{0:T(128)S(1)} %get-tuple-element.169), channel_id=1, replica_groups=mesh['row'=8,'col'=4] {'row','col'}, use_global_device_ids=true, to_apply=%region_20.21 | all-reduce | flops 110 | bytes 880 | tf_op jit(solution)/shard_map/psum | solution.py:80
  193.3 0.1 fusion.13
  193.4 0.0 copy-start.3
  193.4 0.2 fusion.12
  193.6 0.5 log_multiply_fusion.3
  194.1 0.2 multiply_reduce_fusion
  194.3 0.5 div.61
  194.9 0.0 copy-done.3
  (10 shorter events, 0.1 us)
Async XLA Ops:
  7.2 33.1 %all-gather.3.cloned.1.call-start = ((), (), s32[]{:S(2)}) async-start(), calls=%async_computation.1 | async-start | bytes 1310720 | tf_op jit(solution)/shard_map/all_gather | solution.py:66
  7.9 61.5 %all-gather.5.cloned.1.call-start = ((), (), s32[]{:S(2)}) async-start(), calls=%async_computation.2 | async-start | bytes 2359296 | tf_op jit(solution)/shard_map/all_gather | solution.py:69
  8.6 103.0 %reduce-scatter.2.cloned.1.call-start = ((), (), s32[]{:S(2)}) async-start(), calls=%async_computation.3 | async-start | bytes 40960 | tf_op jit(solution)/shard_map/reduce_scatter | solution.py:75
  69.4 2.2 %copy-start = (bf16[1024,1024]{1,0:T(8,128)(2,1)S(1)}, bf16[1024,1024]{1,0:T(8,128)(2,1)}, u32[]{:S(2)}) copy-start(bf16[1024,1024]{1,0:T(8,128)(2,1)} %all-gather.5.cloned.1.call-done) | copy-start | bytes 6291460
  69.4 2.9 %copy-start.1 = (bf16[512,1024]{1,0:T(8,128)(2,1)S(1)}, bf16[512,1024]{1,0:T(8,128)(2,1)}, u32[]{:S(2)}) copy-start(bf16[512,1024]{1,0:T(8,128)(2,1)} %all-gather.3.cloned.1.call-done) | copy-start | bytes 3145732
  91.7 0.6 copy-start.2
  193.4 1.5 copy-start.3
Sparse Core Ops, SparseCore 0:
  9.5 30.6 all-gather.2
  42.2 27.1 all-gather.4
  92.5 19.1 reduce-scatter.1
where the time goes:
time: 202 us; the launch traced here: 201 us
  blocking collectives  79.4 us (39%)
  waiting for transfers between devices  77.6 us (38%)
  matrix products  17.6 us (9%)
  between operations  13.8 us (7%)
  other arithmetic  10.3 us (5%)
  local copies, waits for them, and re-layouts  2.49 us (1%)
    psum x1, blocking collectives, on_device(): lax.psum((jnp.sum(weights, axis=1), jnp.sum(degree, axis=1)), ('row', 'co...  40.9 us
    pmax x1, blocking collectives, on_device(): peak = lax.pmax(jnp.max(degree, axis=1), ('row', 'col'))  38.4 us
    all_gather x1, waiting for transfers between devices, on_device(): left_genes = lax.all_gather(expression, 'col', axis=0, tiled=True)  30.9 us
    all_gather x1, waiting for transfers between devices, on_device(): lax.all_gather(expression, 'row', axis=0, tiled=True)  26 us
    reduce_scatter x1, waiting for transfers between devices, on_device(): lax.psum_scatter(row_totals, 'col', scatter_dimension=1, tiled=True)  19.3 us
    dot_general x2, matrix products, one_block(): lax.dot_general(row_block, right_genes, (((1,), (1,)), ((), ())), preferr...  17.6 us
  transfers between devices with their start and end apart: 3, of which 3 were waited for; matrix products, arithmetic and copies ran while one was open for 2% of the time, Pallas kernels for 0%

commit v1 on v0

--- a/solution.py
+++ b/solution.py
@@ -63,7 +63,12 @@
         jnp.zeros((len(row_list), row_width), jnp.float32),
         jnp.zeros((max(len(col_list), 1), column_width), jnp.float32),
     )
-    left_genes = lax.all_gather(expression, "col", axis=0, tiled=True)
+    ring = [expression]
+    for hop in range(3):
+        ring.append(lax.ppermute(ring[-1], "col", [(dev, (dev + 1) % 4) for dev in range(4)]))
+    left_genes = jnp.roll(
+        jnp.concatenate(ring[::-1], axis=0), (lax.axis_index("col") + 1) * ring[0].shape[0], axis=0
+    )
     row_totals, column_totals = block_sums(
         left_genes,
         lax.all_gather(expression, "row", axis=0, tiled=True),

time: 202 us -> 173 us (0.86)
  waiting for transfers between devices: 77.6 us -> 46.9 us
  starting transfers between devices: 0.11 us -> 3.19 us
  other arithmetic: 10.3 us -> 7.89 us
    all_gather x1 -> x0, waiting for transfers between devices: 30.9 us -> none  [on_device(): left_genes = lax.all_gather(expression, 'col', axis=0, tiled=True)]
    ppermute x0 -> x3, waiting for transfers between devices: none -> 25.6 us  [on_device(): lax.ppermute(ring[-1], 'col', [(dev, (dev + 1) % 4) for dev in range(4)])]
    all_gather x1, waiting for transfers between devices: 26 us -> 1.29 us  [on_device(): lax.all_gather(expression, 'row', axis=0, tiled=True)]
    ppermute x0 -> x3, starting transfers between devices: none -> 3.11 us  [on_device(): lax.ppermute(ring[-1], 'col', [(dev, (dev + 1) % 4) for dev in range(4)])]
  transfers between devices with their start and end apart: 3 -> 5, of which waited for: 3 -> 5; matrix products, arithmetic and copies ran while one was open for 2% -> 1% of each run, Pallas kernels for 0% -> 0%
where the time goes in v1:
time: 173 us
  blocking collectives  79.3 us (46%)
  waiting for transfers between devices  46.9 us (27%)
  matrix products  17.6 us (10%)
  between operations  14.2 us (8%)
  other arithmetic  7.89 us (5%)
  local copies, waits for them, and re-layouts  3.6 us (2%)
  starting transfers between devices  3.19 us (2%)
    psum x1, blocking collectives, on_device(): lax.psum((jnp.sum(weights, axis=1), jnp.sum(degree, axis=1)), ('row', 'co...  40.9 us
    pmax x1, blocking collectives, on_device(): peak = lax.pmax(jnp.max(degree, axis=1), ('row', 'col'))  38.4 us
    ppermute x3, waiting for transfers between devices, on_device(): lax.ppermute(ring[-1], 'col', [(dev, (dev + 1) % 4) for dev in range(4)])  25.6 us
    reduce_scatter x1, waiting for transfers between devices, on_device(): lax.psum_scatter(row_totals, 'col', scatter_dimension=1, tiled=True)  19.3 us
    dot_general x2, matrix products, one_block(): lax.dot_general(row_block, right_genes, (((1,), (1,)), ((), ())), preferr...  17.6 us
  transfers between devices with their start and end apart: 5, of which 5 were waited for; matrix products, arithmetic and copies ran while one was open for 1% of the time, Pallas kernels for 0%

profile of v1, /device:TPU:0, one launch (start us, length us, event | category | flops | bytes accessed | tf_op | source)
XLA Modules:
  0.0 172.7 jit_solution(12598485530744555915)
XLA Ops:
  7.2 0.0 copy-start.1
  7.2 0.0 all-gather.2.cloned.1.call-start
  7.2 0.7 all-gather.2.cloned.1.call-update
  7.9 0.0 reduce-scatter.2.cloned.1.call-start
  8.0 3.1 %collective-permute-start = (bf16[128,1024]{1,0:T(8,128)(2,1)}, bf16[128,1024]{1,0:T(8,128)(2,1)S(1)}, u32[]{:S(2)}, u32[]{:S(2)}) collective-permute-start(bf16[128,1024]{1,0:T(8,128)(2,1)} %param.4), channel_id=1, source_target_pairs={{0,1},{1,2},{2,3},{3,0},{4,5},{5,6},{6,7},{7,4},{8,9},{9,10},{10,1... | collective-permute-start | bytes 786440 | tf_op jit(solution)/shard_map/ppermute | solution.py:68
  11.1 8.5 %collective-permute-done = bf16[128,1024]{1,0:T(8,128)(2,1)S(1)} collective-permute-done((bf16[128,1024]{1,0:T(8,128)(2,1)}, bf16[128,1024]{1,0:T(8,128)(2,1)S(1)}, u32[]{:S(2)}, u32[]{:S(2)}) %collective-permute-start) | collective-permute-done | bytes 262176 | tf_op jit(solution)/shard_map/ppermute | solution.py:68
  19.6 0.0 collective-permute-start.1
  19.6 9.3 %collective-permute-done.1 = bf16[128,1024]{1,0:T(8,128)(2,1)S(1)} collective-permute-done((bf16[128,1024]{1,0:T(8,128)(2,1)S(1)}, bf16[128,1024]{1,0:T(8,128)(2,1)S(1)}, u32[]{:S(2)}, u32[]{:S(2)}) %collective-permute-start.1) | collective-permute-done | bytes 262176 | tf_op jit(solution)/shard_map/ppermute | solution.py:68
  28.9 0.0 collective-permute-start.2
  28.9 0.7 convert_element_type.9
  29.5 7.8 %collective-permute-done.2 = bf16[128,1024]{1,0:T(8,128)(2,1)S(1)} collective-permute-done((bf16[128,1024]{1,0:T(8,128)(2,1)S(1)}, bf16[128,1024]{1,0:T(8,128)(2,1)S(1)}, u32[]{:S(2)}, u32[]{:S(2)}) %collective-permute-start.2) | collective-permute-done | bytes 262176 | tf_op jit(solution)/shard_map/ppermute | solution.py:68
  37.4 1.0 constant_dynamic-update-slice_fusion.4
  38.4 0.0 copy-done.1
  38.5 0.2 convert_reduce_fusion.1
  38.7 0.4 fusion.10
  39.1 1.3 all-gather.2.cloned.1.call-done
  40.4 0.0 copy-start
  40.4 2.1 %convert_reduce_fusion = f32[1024]{0:T(1024)S(1)} fusion(bf16[1024,1024]{1,0:T(8,128)(2,1)} %all-gather.2.cloned.1.call-done), kind=kLoop, calls=%fused_computation.20 | loop fusion | flops 2096128 | bytes 2101248 | tf_op jit(solution)/shard_map/reduce_sum | solution.py:11
  42.5 0.1 copy-done
  42.6 0.7 fusion.8
  43.3 19.4 %while.13 = (s32[]{:T(128)}, f32[10,512]{1,0:T(8,128)S(1)}, f32[10]{0:T(128)S(1)}, bf16[512,1024]{1,0:T(8,128)(2,1)S(1)}, bf16[1024,1024]{1,0:T(8,128)(2,1)S(1)}...) while((s32[]{:T(128)}, f32[10,512]{1,0:T(8,128)S(1)}, ...), condition=%wide.region_15.16_spmd, body=%wide.region_4.15_spmd.sunk | while | flops 543686656 | bytes 2715955 | solution.py:51
  43.4 0.1 dynamic_slice.46
  43.4 0.1 dynamic_slice.47
  43.5 0.7 fusion.20
  44.2 8.8 %exponential_reduce_fusion.11 = (f32[256]{0:T(256)S(1)}, f32[256]{0:T(256)S(1)}, f32[256]{0:T(256)S(1)}, f32[256]{0:T(256)S(1)}, f32[256]{0:T(256)S(1)}, /*index...) fusion(f32[]{:T(128)} %bitcast.43, f32[]{:T(128)} %bitcast.44, ...), kind=kOutput, calls=%fused_computation.6.clone.1 | convolution fusion | flops 543684096 | bytes 2641964 | tf_op jit(solution)/shard_map/while/body/eval_jaxpr/dot_general | solution.py:35
  53.0 0.1 stack.78
  53.1 0.1 dynamic_slice.46
  53.1 0.1 dynamic_slice.47
  53.2 0.7 fusion.20
  53.9 8.8 %exponential_reduce_fusion.11 = (f32[256]{0:T(256)S(1)}, f32[256]{0:T(256)S(1)}, f32[256]{0:T(256)S(1)}, f32[256]{0:T(256)S(1)}, f32[256]{0:T(256)S(1)}, /*index...) fusion(f32[]{:T(128)} %bitcast.43, f32[]{:T(128)} %bitcast.44, ...), kind=kOutput, calls=%fused_computation.6.clone.1 | convolution fusion | flops 543684096 | bytes 2641964 | tf_op jit(solution)/shard_map/while/body/eval_jaxpr/dot_general | solution.py:35
  62.7 0.1 stack.78
  62.7 0.0 copy-start.2
  62.8 0.6 copy-done.2
  63.3 0.0 reduce-scatter.2.cloned.1.call-update
  63.4 19.3 %reduce-scatter.2.cloned.1.call-done = f32[10,128]{1,0:T(8,128)} async-done(((f32[10,512]{1,0:T(8,128)}), f32[10,128]{1,0:T(8,128)}) %reduce-scatter.2.cloned.1.call-update) | async-done | bytes 5136 | tf_op jit(solution)/shard_map/reduce_scatter | solution.py:80
  82.7 0.8 fusion.14
  83.5 38.4 %pmax.7 = f32[10]{0:T(128)S(1)} all-reduce(f32[10]{0:T(128)S(1)} %get-tuple-element.170), channel_id=1, replica_groups=mesh['row'=8,'col'=4] {'row','col'}, use_global_device_ids=true, to_apply=%region_18.19 | all-reduce | flops 10 | bytes 80 | tf_op jit(solution)/shard_map/pmax | solution.py:81
  121.9 1.3 add_clamp_fusion
  123.2 0.1 maximum_reduce_fusion
  123.4 40.9 %all-reduce = (f32[10,10]{1,0:T(8,128)S(1)}, f32[10]{0:T(128)S(1)}) all-reduce(f32[10,10]{1,0:T(8,128)S(1)} %maximum_reduce_fusion, f32[10]{0:T(128)S(1)} %get-tuple-element.169), channel_id=1, replica_groups=mesh['row'=8,'col'=4] {'row','col'}, use_global_device_ids=true, to_apply=%region_20.21 | all-reduce | flops 110 | bytes 880 | tf_op jit(solution)/shard_map/psum | solution.py:85
  164.2 0.1 fusion.13
  164.4 0.0 copy-start.3
  164.4 0.2 fusion.12
  164.6 0.5 log_multiply_fusion.3
  165.1 0.2 multiply_reduce_fusion
  165.3 0.5 div.61
  165.8 0.0 copy-done.3
  (17 shorter events, 0.2 us)
Async XLA Ops:
  7.2 31.3 %copy-start.1 = (bf16[128,1024]{1,0:T(8,128)(2,1)S(1)}, bf16[128,1024]{1,0:T(8,128)(2,1)}, u32[]{:S(2)}) copy-start(bf16[128,1024]{1,0:T(8,128)(2,1)} %param.4) | copy-start | bytes 786436
  7.2 33.2 %all-gather.2.cloned.1.call-start = ((), (), s32[]{:S(2)}) async-start(), calls=%async_computation.1 | async-start | bytes 2359296 | tf_op jit(solution)/shard_map/all_gather | solution.py:74
  7.9 74.8 %reduce-scatter.2.cloned.1.call-start = ((), (), s32[]{:S(2)}) async-start(), calls=%async_computation.2 | async-start | bytes 40960 | tf_op jit(solution)/shard_map/reduce_scatter | solution.py:80
  8.0 11.6 %collective-permute-start = (bf16[128,1024]{1,0:T(8,128)(2,1)}, bf16[128,1024]{1,0:T(8,128)(2,1)S(1)}, u32[]{:S(2)}, u32[]{:S(2)}) collective-permute-start(bf16[128,1024]{1,0:T(8,128)(2,1)} %param.4), channel_id=1, source_target_pairs={{0,1},{1,2},{2,3},{3,0},{4,5},{5,6},{6,7},{7,4},{8,9},{9,10},{10,1... | collective-permute-start | bytes 786440 | tf_op jit(solution)/shard_map/ppermute | solution.py:68
  19.6 9.3 %collective-permute-start.1 = (bf16[128,1024]{1,0:T(8,128)(2,1)S(1)}, bf16[128,1024]{1,0:T(8,128)(2,1)S(1)}, u32[]{:S(2)}, u32[]{:S(2)}) collective-permute-start(bf16[128,1024]{1,0:T(8,128)(2,1)S(1)} %collective-permute-done), channel_id=1, source_target_pairs={{0,1},{1,2},{2,3},{3,0},{4,5},{5,6},{6,7},{7,4},{8,9},{9,10},{10,1... | collective-permute-start | bytes 786440 | tf_op jit(solution)/shard_map/ppermute | solution.py:68
  28.9 8.4 %collective-permute-start.2 = (bf16[128,1024]{1,0:T(8,128)(2,1)S(1)}, bf16[128,1024]{1,0:T(8,128)(2,1)S(1)}, u32[]{:S(2)}, u32[]{:S(2)}) collective-permute-start(bf16[128,1024]{1,0:T(8,128)(2,1)S(1)} %collective-permute-done.1), channel_id=1, source_target_pairs={{0,1},{1,2},{2,3},{3,0},{4,5},{5,6},{6,7},{7,4},{8,9},{9,10},{10,1... | collective-permute-start | bytes 786440 | tf_op jit(solution)/shard_map/ppermute | solution.py:68
  40.4 2.2 %copy-start = (bf16[1024,1024]{1,0:T(8,128)(2,1)S(1)}, bf16[1024,1024]{1,0:T(8,128)(2,1)}, u32[]{:S(2)}) copy-start(bf16[1024,1024]{1,0:T(8,128)(2,1)} %all-gather.2.cloned.1.call-done) | copy-start | bytes 6291460
  62.7 0.6 copy-start.2
  164.4 1.5 copy-start.3
Sparse Core Ops, SparseCore 0:
  9.9 30.4 all-gather.1
  63.5 19.1 reduce-scatter.1
